TPU v7x, 32 devices: a whole 2x2x4 slice. The times are simulated.
32 devices in a mesh: dp: 4 (over y, core), seq: 8 (over z, x).
Axes of the slice: x: 2, y: 2, z: 4, core: 2. Of those that a mesh axis runs over, the one named last changes fastest.
Arguments:
- queries: bfloat16 [4, 4096, 1024], P('dp', 'seq'), may hold values from -6 to 6
- key_vectors: bfloat16 [4, 4096, 1024], P('dp', 'seq'), may hold values from -6 to 6
- value_vectors: bfloat16 [4, 4096, 2048], P('dp', 'seq'), may hold values from -6 to 6
- grad_output: bfloat16 [4, 4096, 2048], P('dp', 'seq'), may hold values from -0.375 to 0.375
- log_gate: float32 [4, 4096, 1024], P('dp', 'seq'), may hold values from -1 to 0, as said below
- layer_input: bfloat16 [4, 4096, 2048], P('dp', 'seq'), may hold values from -0.0625 to 0.0625
Outputs:
- grad_queries: bfloat16 [4, 4096, 1024], P('dp', 'seq')
- grad_keys: bfloat16 [4, 4096, 1024], P('dp', 'seq')
- grad_values: bfloat16 [4, 4096, 2048], P('dp', 'seq')
- grad_log_gate: float32 [4, 4096, 1024], P('dp', 'seq')
- grad_key_weight: float32 [2048, 1024], P(('dp', 'seq'))
Inputs may be any that keep to these rules, and one draw needn't show every extreme that they name: `log_gate`: every entry is negative.
All inputs are finite; a program needn't handle non-finite values.
Results may differ from a plain program's by a relative error of at most 0.03.
Values sent between devices are 32-bit elements; how exact they have to be, the bound alone decides.
A program may use at most 192 MiB of HBM per device.

v0:
```python
import jax
import jax.numpy as jnp
from jax import lax
from jax.sharding import PartitionSpec as P

HEADS = 4
DK = 256
DV = 512
GROUP = 64


def carried_in(part, axis, combine, identity, reverse):
    count = lax.axis_size(axis)
    place = lax.axis_index(axis)
    ahead = count - 1 - place if reverse else place
    gathered = jax.tree.map(lambda a: lax.all_gather(a, axis), part)
    state = jax.tree.map(lambda a, e: jnp.zeros_like(a) + jnp.asarray(e, a.dtype), part, identity)

    def one(step, state):
        source = count - 1 - step if reverse else step
        return combine(
            state, jax.tree.map(lambda a: lax.dynamic_index_in_dim(a, source, 0, False), gathered)
        )

    return lax.fori_loop(0, ahead, one, state)


def product(pattern, first_op, second_op):
    return jnp.einsum(
        pattern,
        first_op.astype(jnp.bfloat16),
        second_op.astype(jnp.bfloat16),
        preferred_element_type=jnp.float32,
    )


def lower_mask_of():
    return (
        lax.broadcasted_iota(jnp.int32, (GROUP, GROUP), 0)
        >= lax.broadcasted_iota(jnp.int32, (GROUP, GROUP), 1)
    ).astype(jnp.float32)


def chained(earlier, later_part):
    decay_early, state_early = earlier
    decay_late, state_late = later_part
    return (decay_early * decay_late, decay_late[..., None] * state_early + state_late)


def carried(device_decay, forward_state, backward_state):
    identity_pair = (jnp.ones_like(device_decay), jnp.zeros_like(forward_state))
    incoming = carried_in((device_decay, forward_state), "seq", chained, identity_pair, False)[1]
    outgoing = carried_in((device_decay, backward_state), "seq", chained, identity_pair, True)[1]
    return (incoming, outgoing)


def forward_blocks(key_rows, value_rows, cotan_rows, block_cums, start_state, key_scale):
    lower_mask = lower_mask_of()

    def forward_advance(carry_state, block):
        key_part, value_part, cotan_part, cum_part = block
        cum_end = cum_part[-1]
        pair_dot = product("thj,shj->hts", cotan_part, value_part) * lower_mask
        grad_q = (
            key_scale
            * jnp.exp(cum_part)
            * (
                product("thj,hij->thi", cotan_part, carry_state)
                + product("hts,shi->thi", pair_dot, key_part * jnp.exp(-cum_part))
            )
        )
        carry_state = carry_state * jnp.exp(cum_end)[..., None] + product(
            "shi,shj->hij", key_part * jnp.exp(cum_end - cum_part), value_part
        )
        return (carry_state, grad_q)

    return lax.scan(forward_advance, start_state, (key_rows, value_rows, cotan_rows, block_cums))


def backward_blocks(
    query_rows, key_rows, value_rows, cotan_rows, block_cums, start_state, key_scale
):
    lower_mask = lower_mask_of()

    def backward_advance(back_state, block):
        query_part, key_part, value_part, cotan_part, cum_part = block
        cum_end = cum_part[-1]
        query_up = query_part * jnp.exp(cum_part)
        key_down = key_part * jnp.exp(-cum_part)
        key_end = key_part * jnp.exp(cum_end - cum_part)
        scores = key_scale * product("thi,shi->hts", query_up, key_down) * lower_mask
        pair_dot = product("thj,shj->hts", cotan_part, value_part) * lower_mask
        grad_k = key_scale * jnp.exp(-cum_part) * product(
            "hts,thi->shi", pair_dot, query_up
        ) + jnp.exp(cum_end - cum_part) * product("shj,hij->shi", value_part, back_state)
        grad_v = product("hts,thj->shj", scores, cotan_part) + product(
            "shi,hij->shj", key_end, back_state
        )
        back_state = back_state * jnp.exp(cum_end)[..., None] + key_scale * product(
            "thi,thj->hij", query_up, cotan_part
        )
        return (back_state, (grad_k, grad_v))

    return lax.scan(
        backward_advance,
        start_state,
        (query_rows, key_rows, value_rows, cotan_rows, block_cums),
        reverse=True,
    )


def shards(queries, key_vectors, value_vectors, grad_output, log_gate, layer_input):
    length = queries.shape[1]
    blocks = length // GROUP
    key_scale = DK ** (-0.5)

    def as_blocks(array, width):
        return array[0].reshape(blocks, GROUP, HEADS, width)

    query_rows = as_blocks(queries, DK)
    key_rows = as_blocks(key_vectors, DK)
    value_rows = as_blocks(value_vectors, DV)
    cotan_rows = as_blocks(grad_output, DV)
    block_cums = jnp.cumsum(as_blocks(log_gate, DK), axis=1)
    block_ends = block_cums[:, -1]
    offsets = jnp.cumsum(block_ends, axis=0) - block_ends
    device_cum = block_cums + offsets[:, None]
    total_log = offsets[-1] + block_ends[-1]
    device_decay = jnp.exp(total_log)
    to_end = jnp.exp(total_log - device_cum)
    from_start = jnp.exp(device_cum)
    forward_state = product("nchi,nchj->hij", key_rows * to_end, value_rows)
    backward_state = key_scale * product("nchi,nchj->hij", query_rows * from_start, cotan_rows)
    incoming, outgoing = carried(device_decay, forward_state, backward_state)
    grad_q = forward_blocks(key_rows, value_rows, cotan_rows, block_cums, incoming, key_scale)[1]
    grad_k, grad_v = backward_blocks(
        query_rows, key_rows, value_rows, cotan_rows, block_cums, outgoing, key_scale
    )[1]
    log_drift = query_rows.astype(jnp.float32) * grad_q - key_rows.astype(jnp.float32) * grad_k
    block_sums = jnp.sum(log_drift, axis=1)
    after_sums = jnp.cumsum(block_sums[::-1], axis=0)[::-1] - block_sums
    local_tail = lax.cumsum(log_drift, axis=1, reverse=True) + after_sums[:, None]
    device_sum = jnp.sum(block_sums, axis=0)
    tail_sum = carried_in(device_sum, "seq", jnp.add, jnp.zeros_like(device_sum), True)
    grad_log_gate = (local_tail + tail_sum).reshape(1, length, HEADS * DK)
    keys_low = grad_k.reshape(length, HEADS * DK).astype(jnp.bfloat16)
    input_rows = layer_input[0]
    grad_key_weight = lax.psum_scatter(
        lax.dot_general(
            input_rows, keys_low, (((0,), (0,)), ((), ())), preferred_element_type=jnp.float32
        ),
        ("dp", "seq"),
        scatter_dimension=0,
        tiled=True,
    )
    grad_queries = grad_q.reshape(1, length, HEADS * DK).astype(jnp.bfloat16)
    grad_keys = keys_low.reshape(1, length, HEADS * DK)
    grad_values = grad_v.reshape(1, length, HEADS * DV).astype(jnp.bfloat16)
    return (grad_queries, grad_keys, grad_values, grad_log_gate, grad_key_weight)


def solution(mesh):
    placed = (
        P("dp", "seq", None),
        P("dp", "seq", None),
        P("dp", "seq", None),
        P("dp", "seq", None),
        P("dp", "seq", None),
        P("dp", "seq", None),
    )
    return jax.shard_map(
        shards,
        mesh=mesh,
        in_specs=placed,
        out_specs=(
            P("dp", "seq", None),
            P("dp", "seq", None),
            P("dp", "seq", None),
            P("dp", "seq", None),
            P(("dp", "seq"), None),
        ),
        check_vma=False,
    )
```

profile of v0, /device:TPU:1, one launch (start us, length us, event | category | flops | bytes accessed | tf_op | source)
XLA Modules:
  0.0 680.0 jit_solution(8803694880820029048)
XLA Ops:
  7.2 3.3 reshape_squeeze.15
  14.6 4.5 reshape_squeeze.18
  21.0 7.7 %bitcast_multiply_fusion = f32[4,256,512]{2,1,0:T(8,128)} fusion(bf16[8,64,4,512]{3,2,1,0:T(4,128)(2,1)} %reshape_squeeze.18, f32[8,64,4,256]{3,0,1,2:T(8,128)} %copy-done.4, f32[8,4,256]{2,0,1:T(8,128)S(1)} %fusion.119, bf16[8,64,4,256]{3,2,1,0:T(4,128)(2,1)S(1)} %reshape_squeeze.19), kind=kOutput, calls=%fused_computation.117 | convolution fusion | flops 539492352 | bytes 7372800 | tf_op jit(solution)/shard_map/nchi,nchj->hij/dot_general | solution.py:29
  31.4 4.9 reshape_squeeze.17
  36.3 7.4 %fusion.107 = f32[4,256,512]{2,1,0:T(8,128)} fusion(bf16[8,64,4,512]{3,2,1,0:T(4,128)(2,1)} %reshape_squeeze.17, f32[8,64,4,256]{3,0,1,2:T(8,128)} %copy-done.4, f32[8,4,256]{2,0,1:T(8,128)S(1)} %fusion.119, f32[4,256]{1,0:T(4,128)S(1)} %bitcast.292, bf16[8,64,4,256]{3,2,1,0:T(4,128)(2,1)S(1)} %reshape_squeeze.16), kind=kOutput, calls=%fused_computation.124 | convolution fusion | flops 539492352 | bytes 7376896 | tf_op jit(solution)/shard_map/nchi,nchj->hij/dot_general | solution.py:29
  44.0 4.3 copy.70
  54.8 27.1 %all_gather.24 = f32[8,4,256]{2,1,0:T(4,128)S(1)} all-gather(f32[1,4,256]{2,1,0:T(4,128)S(1)} %copy.67), channel_id=1, replica_groups=mesh['dp'=4,'seq'=8] {'seq'}, dimensions={0}, use_global_device_ids=true | all-gather | bytes 36864 | tf_op jit(solution)/shard_map/all_gather | solution.py:16
  81.9 175.7 %all-gather.9.cloned.1.call-done = f32[32,256,512]{2,1,0:T(8,128)} async-done(((f32[4,256,512]{2,1,0:T(8,128)}), f32[32,256,512]{2,1,0:T(8,128)}) %all-gather.9.cloned.1.call-update) | async-done | bytes 16777232 | tf_op jit(solution)/shard_map/all_gather | solution.py:16
  259.2 27.5 %while.72 = (s32[]{:T(128)}, f32[4,256,512]{2,1,0:T(8,128)}, s32[]{:T(128)}, f32[8,4,256]{2,1,0:T(4,128)S(1)}, f32[8,4,256,512]{3,2,1,0:T(8,128)}, /*index=5*/s32[]{:T(128)}, s32[]{:T(128)}, s32[]{:T(128)}, s32[]{:T(128)}) while((s32[]{:T(128)}, f32[4,256,512]{2,1,0:T(8,128)}, s32[]{:T(128)}, f32[8,4,256]{2,1,0:T(4,128)S(1)}, ...), condition=%wide.region_7.8_spmd, body=%wide.region_6.7_spmd.sunk | while | flops 1048582 | bytes 6303891 | solution.py:25
  259.2 3.8 bitcast_add_fusion.9
  263.0 3.8 bitcast_add_fusion.9
  266.8 4.5 bitcast_add_fusion.9
  271.4 3.8 bitcast_add_fusion.9
  275.2 3.8 bitcast_add_fusion.9
  279.0 3.9 bitcast_add_fusion.9
  282.9 3.8 bitcast_add_fusion.9
  289.8 116.8 %while.75 = (s32[]{:T(128)}, f32[4,256,512]{2,1,0:T(8,128)}, f32[8,64,4,256]{3,1,2,0:T(8,128)}, bf16[8,64,4,512]{3,1,2,0:T(8,128)(2,1)}, f32[8,64,4,256]{3,2,1,0...) while((s32[]{:T(128)}, f32[4,256,512]{2,1,0:T(8,128)}, ...), condition=%wide.region_9.10_spmd.clone.clone, body=%wide.region_8.9_spmd.clone.clone.sunk | while | flops 256000000 | bytes 15462061 | solution.py:104
  298.2 2.7 fusion.182
  300.8 3.5 multiply_add_fusion.5
  309.1 2.2 fusion.180
  312.7 2.7 fusion.182
  315.4 3.5 multiply_add_fusion.5
  323.7 2.2 fusion.180
  327.3 2.7 fusion.182
  329.9 3.5 multiply_add_fusion.5
  341.8 2.7 fusion.182
  344.4 3.8 multiply_add_fusion.5
  350.0 2.3 fusion.178
  356.8 2.7 fusion.182
  359.4 3.5 multiply_add_fusion.5
  371.3 2.7 fusion.182
  374.0 3.5 multiply_add_fusion.5
  382.3 2.2 fusion.180
  385.9 2.7 fusion.182
  388.6 3.5 multiply_add_fusion.5
  393.7 2.2 fusion.178
  396.9 2.2 fusion.180
  400.5 2.7 fusion.182
  403.1 3.5 multiply_add_fusion.5
  409.4 5.6 convolution_bitcast_fusion.6
  415.0 9.3 %copy.93 = f32[2048,1024]{1,0:T(8,128)} copy(f32[2048,1024]{0,1:T(8,128)} %convolution_bitcast_fusion.6) | data formatting | bytes 16777216
  425.9 59.4 %all-gather.7.cloned.1.call-done = f32[32,256,512]{2,1,0:T(8,128)} async-done(((f32[4,256,512]{2,1,0:T(8,128)}), f32[32,256,512]{2,1,0:T(8,128)}) %all-gather.7.cloned.1.call-update) | async-done | bytes 16777232 | tf_op jit(solution)/shard_map/all_gather | solution.py:16
  488.5 76.2 %while.74 = (s32[]{:T(128)}, f32[4,256,512]{2,1,0:T(8,128)}, f32[8,64,4,256]{3,1,2,0:T(8,128)}, f32[8,64,4,256]{3,2,1,0:T(4,128)}, bf16[8,64,4,256]{3,1,2,0:T(8,...) while((s32[]{:T(128)}, f32[4,256,512]{2,1,0:T(8,128)}, ...), condition=%wide.region_5.6_spmd.clone, body=%wide.region_4.5_spmd.clone.sunk | while | flops 161718272 | bytes 9772669 | solution.py:77
  494.4 3.6 multiply_add_fusion.4
  503.9 3.6 multiply_add_fusion.4
  513.4 3.6 multiply_add_fusion.4
  518.0 2.2 convolution_bitcast_fusion.9
  523.0 3.6 multiply_add_fusion.4
  527.6 2.2 convolution_bitcast_fusion.9
  532.5 3.6 multiply_add_fusion.4
  542.0 3.6 multiply_add_fusion.4
  546.6 2.2 convolution_bitcast_fusion.9
  551.6 3.6 multiply_add_fusion.4
  561.1 3.6 multiply_add_fusion.4
  567.2 6.6 fusion.121
  574.0 3.8 broadcast_add_fusion.1
  577.8 2.7 copy.86
  580.5 3.3 add.170
  583.8 50.8 %all-gather.3 = f32[8,4,256]{2,1,0:T(4,128)S(1)} all-gather(f32[1,4,256]{2,1,0:T(4,128)S(1)} %bitcast.290), channel_id=4, replica_groups=mesh['dp'=4,'seq'=8] {'seq'}, dimensions={0}, use_global_device_ids=true | all-gather | bytes 36864 | tf_op jit(solution)/shard_map/all_gather | solution.py:16
  636.9 2.6 convert_element_type.171
  639.4 4.6 copy.83
  644.0 4.5 convert_element_type.177
  648.4 3.3 broadcast_add_fusion
  651.7 21.8 %reduce-scatter.4.cloned.1.call-done = f32[64,1024]{1,0:T(8,128)} async-done(((f32[2048,1024]{1,0:T(8,128)}), f32[64,1024]{1,0:T(8,128)}) %reduce-scatter.4.cloned.1.call-update) | async-done | bytes 262160
  (163 shorter events, 127.1 us)
Async XLA Ops:
  7.2 402.3 %copy-start = (bf16[1,512,2048]{2,1,0:T(8,128)(2,1)S(1)}, bf16[1,512,2048]{2,1,0:T(8,128)(2,1)}, u32[]{:S(2)}) copy-start(bf16[1,512,2048]{2,1,0:T(8,128)(2,1)} %param.21) | copy-start | bytes 6291460
  7.2 250.4 %all-gather.9.cloned.1.call-start = ((), (), s32[]{:S(2)}) async-start(), calls=%async_computation.2 | async-start | bytes 18874368 | tf_op jit(solution)/shard_map/all_gather | solution.py:16
  12.5 1.3 copy-start.4
  21.0 7.7 %copy-start.7 = (bf16[8,64,4,256]{3,2,1,0:T(4,128)(2,1)}, bf16[8,64,4,256]{3,2,1,0:T(4,128)(2,1)S(1)}, u32[]{:S(2)}) copy-start(bf16[8,64,4,256]{3,2,1,0:T(4,128)(2,1)S(1)} %reshape_squeeze.19) | copy-start | bytes 3145732
  28.7 456.6 %all-gather.7.cloned.1.call-start = ((), (), s32[]{:S(2)}) async-start(), calls=%async_computation.1 | async-start | bytes 18874368 | tf_op jit(solution)/shard_map/all_gather | solution.py:16
  31.4 16.8 %copy-start.2 = (bf16[8,64,4,256]{3,2,1,0:T(4,128)(2,1)}, bf16[8,64,4,256]{3,2,1,0:T(4,128)(2,1)S(1)}, u32[]{:S(2)}) copy-start(bf16[8,64,4,256]{3,2,1,0:T(4,128)(2,1)S(1)} %reshape_squeeze.16) | copy-start | bytes 3145732
  43.7 629.7 %reduce-scatter.4.cloned.1.call-start = ((), (), s32[]{:S(2)}) async-start(), calls=%async_computation.3 | async-start | bytes 8650752
  48.3 2.0 copy-start.6
  50.2 1.8 copy-start.5
  564.7 2.2 copy-start.1
  564.7 2.5 copy-start.3
Sparse Core Ops, SparseCore 0:
  28.8 228.7 all-gather.8
  259.7 225.5 all-gather.6
  488.2 185.2 reduce-scatter.3
where the time goes:
time: 684 us; the launch traced here: 680 us
  waiting for transfers between devices  257 us (38%)
  matrix products  179 us (26%)
  local copies, waits for them, and re-layouts  102 us (15%)
  blocking collectives  77.9 us (11%)
  other arithmetic  49.4 us (7%)
  between operations  13.9 us (2%)
    all_gather x2, waiting for transfers between devices, carried_in(): gathered = jax.tree.map(lambda a: lax.all_gather(a, axis), part)  235 us
    dot_general x66, matrix products, product(): jnp.einsum(pattern, first_op.astype(jnp.bfloat16), second_op.astype(jnp.b...  174 us
    all_gather x2, blocking collectives, carried_in(): gathered = jax.tree.map(lambda a: lax.all_gather(a, axis), part)  77.9 us
    add x7, other arithmetic, chained(): decay_late[..., None] * state_early + state_late  27.5 us
    dynamic_slice x24, local copies, waits for them, and re-layouts, forward_blocks(): lax.scan(forward_advance, start_state, (key_rows, value_rows, cotan_rows,...  23.1 us
    unnamed x4, waiting for transfers between devices  21.8 us
    unnamed x24, local copies, waits for them, and re-layouts  21.5 us
    another operation x5, local copies, waits for them, and re-layouts, as_blocks(): return array[0].reshape(blocks, GROUP, HEADS, width)  16.4 us
  transfers between devices with their start and end apart: 3, of which 3 were waited for; matrix products, arithmetic and copies ran while one was open for 45% of the time, Pallas kernels for 0%

commit v1 on v0

v1 whole, which is shorter than its diff:
```python
import functools

import jax
import jax.numpy as jnp
from jax import lax
from jax.experimental import pallas as pl
from jax.experimental.pallas import tpu as pltpu
from jax.sharding import PartitionSpec as P

HEADS = 4
DK = 256
DV = 512
ROWS = 64
NT = (((1,), (1,)), ((), ()))
TN = (((0,), (0,)), ((), ()))
NN = (((1,), (0,)), ((), ()))


def mm(first_op, second_op, dims):
    return lax.dot_general(
        first_op.astype(jnp.bfloat16),
        second_op.astype(jnp.bfloat16),
        dims,
        preferred_element_type=jnp.float32,
    )


def block_of(length):
    return 128 if length % 128 == 0 else 64


def triangle(size, lower):
    row = lax.broadcasted_iota(jnp.int32, (size, size), 0)
    col = lax.broadcasted_iota(jnp.int32, (size, size), 1)
    return (row >= col) if lower else (row <= col)


def exact_sum(ones, values):
    high = values.astype(jnp.bfloat16)
    rest = values - high.astype(jnp.float32)
    middle = rest.astype(jnp.bfloat16)
    low = (rest - middle.astype(jnp.float32)).astype(jnp.bfloat16)
    return mm(ones, high, NN) + (mm(ones, middle, NN) + mm(ones, low, NN))


def states_kernel(q_ref, k_ref, v_ref, g_ref, lg_ref, decay_ref, f_ref, b_ref):
    length = q_ref.shape[0]
    size = block_of(length)
    ones = triangle(size, True).astype(jnp.bfloat16)
    base = jnp.zeros((1, DK), jnp.float32)
    cums = []
    for n in range(length // size):
        part = exact_sum(ones, lg_ref[n * size : (n + 1) * size, :]) + base
        base = part[size - 1 :, :]
        cums.append(part)
    cum = jnp.concatenate(cums, axis=0)
    decay_ref[...] = jnp.broadcast_to(jnp.exp(base), decay_ref.shape)
    key_end = k_ref[...].astype(jnp.float32) * jnp.exp(base - cum)
    query_up = q_ref[...].astype(jnp.float32) * jnp.exp(cum)
    f_ref[...] = mm(v_ref[...], key_end, TN)
    b_ref[...] = DK**-0.5 * mm(g_ref[...], query_up, TN)


def chain_kernel(
    count, decay_ref, f_ref, b_ref, fin_ref, bin_ref, f_out, b_out, f_send, f_recv, b_send, b_recv
):
    place = lax.axis_index("seq")
    right = lax.rem(place + 1, count)
    left = lax.rem(place + count - 1, count)
    chunks = f_ref.shape[0] // ROWS
    per_head = chunks // HEADS
    barrier = pltpu.get_barrier_semaphore()
    for peer in (left, right):
        pl.semaphore_signal(
            barrier, inc=1, device_id={"seq": peer}, device_id_type=pl.DeviceIdType.MESH
        )
    pl.semaphore_wait(barrier, 2)

    def copy(c, out, into, send, recv, peer):
        rows = pl.ds(pl.multiple_of(c * ROWS, ROWS), ROWS)
        return pltpu.make_async_remote_copy(
            src_ref=out.at[rows],
            dst_ref=into.at[rows],
            send_sem=send.at[c],
            recv_sem=recv.at[c],
            device_id={"seq": peer},
            device_id_type=pl.DeviceIdType.MESH,
        )

    def advance(c, own, out, into, send, recv, peer, is_first, is_last):
        rows = pl.ds(pl.multiple_of(c * ROWS, ROWS), ROWS)

        @pl.when(is_first)
        def _():
            into[rows, :] = jnp.zeros((ROWS, DK), jnp.float32)

        @pl.when(jnp.logical_not(is_first))
        def _():
            copy(c, out, into, send, recv, peer).wait_recv()

        @pl.when(jnp.logical_not(is_last))
        def _():
            decay = decay_ref[pl.ds((c // per_head) * 8, 8), :][0:1, :]
            out[rows, :] = decay * into[rows, :] + own[rows, :]
            copy(c, out, into, send, recv, peer).start()

    at_low, at_high = place == 0, place == count - 1

    def step(t, _):
        ahead = t - place
        back = t - (count - 1 - place)

        @pl.when((ahead >= 0) & (ahead < chunks))
        def _():
            advance(ahead, f_ref, f_out, fin_ref, f_send, f_recv, right, at_low, at_high)

        @pl.when((back >= 0) & (back < chunks))
        def _():
            advance(back, b_ref, b_out, bin_ref, b_send, b_recv, left, at_high, at_low)

        return 0

    lax.fori_loop(0, chunks + count - 1, step, 0)

    def drain(c, _):
        @pl.when(jnp.logical_not(at_high))
        def _():
            copy(c, f_out, fin_ref, f_send, f_recv, right).wait_send()

        @pl.when(jnp.logical_not(at_low))
        def _():
            copy(c, b_out, bin_ref, b_send, b_recv, left).wait_send()

        return 0

    lax.fori_loop(0, chunks, drain, 0)


def grads_kernel(
    q_ref, k_ref, v_ref, g_ref, lg_ref, fin_ref, bin_ref, dq_ref, dk_ref, dv_ref, gate_ref, dq_full
):
    length = q_ref.shape[0]
    size = block_of(length)
    scale = DK**-0.5
    lower = triangle(size, True)
    sum_down = lower.astype(jnp.bfloat16)
    sum_up = triangle(size, False).astype(jnp.bfloat16)
    state = fin_ref[...]
    back = bin_ref[...]
    kept = []
    for n in range(length // size):
        at = slice(n * size, (n + 1) * size)
        cum = exact_sum(sum_down, lg_ref[at, :])
        end = cum[size - 1 :, :]
        middle = cum[size // 2 - 1 : size // 2, :]
        rise = jnp.exp(cum - middle)
        fall = jnp.exp(middle - cum)
        key = k_ref[at, :].astype(jnp.float32)
        pair = jnp.where(lower, mm(g_ref[at, :], v_ref[at, :], NT), 0.0).astype(jnp.bfloat16)
        dq = scale * (
            jnp.exp(cum) * mm(g_ref[at, :], state, NN) + rise * mm(pair, key * fall, NN)
        )
        dq_full[at, :] = dq
        dq_ref[at, :] = dq.astype(jnp.bfloat16)
        state = state * jnp.exp(end) + mm(v_ref[at, :], key * jnp.exp(end - cum), TN)
        kept.append((cum, pair))
    tail = jnp.sum(state * back, axis=0, keepdims=True)
    for n in reversed(range(length // size)):
        at = slice(n * size, (n + 1) * size)
        cum, pair = kept[n]
        end = cum[size - 1 :, :]
        middle = cum[size // 2 - 1 : size // 2, :]
        rise = jnp.exp(cum - middle)
        fall = jnp.exp(middle - cum)
        to_end = jnp.exp(end - cum)
        query = q_ref[at, :].astype(jnp.float32)
        key = k_ref[at, :].astype(jnp.float32)
        query_rise = (query * rise).astype(jnp.bfloat16)
        scores = jnp.where(lower, scale * mm(query_rise, key * fall, NT), 0.0)
        dk = scale * fall * mm(pair, query_rise, TN) + to_end * mm(v_ref[at, :], back, NN)
        dv = mm(scores, g_ref[at, :], TN) + mm(key * to_end, back, NT)
        dk_ref[at, :] = dk.astype(jnp.bfloat16)
        dv_ref[at, :] = dv.astype(jnp.bfloat16)
        sums = exact_sum(sum_up, query * dq_full[at, :] - key * dk) + tail
        gate_ref[at, :] = sums
        tail = sums[0:1, :]
        back = back * jnp.exp(end) + scale * mm(
            g_ref[at, :], query * jnp.exp(cum), TN
        )


def shards(count, queries, key_vectors, value_vectors, grad_output, log_gate, layer_input):
    length = queries.shape[1]
    f32, bf16 = jnp.float32, jnp.bfloat16
    thin = pl.BlockSpec((length, DK), lambda h: (0, h))
    wide = pl.BlockSpec((length, DV), lambda h: (0, h))
    carry = pl.BlockSpec((DV, DK), lambda h: (h, 0))
    rows = (queries[0], key_vectors[0], value_vectors[0], grad_output[0], log_gate[0])
    work = length * DK * DV * HEADS
    decay, forward, backward = pl.pallas_call(
        states_kernel,
        grid=(HEADS,),
        in_specs=[thin, thin, wide, wide, thin],
        out_specs=[pl.BlockSpec((8, DK), lambda h: (h, 0)), carry, carry],
        out_shape=[
            jax.ShapeDtypeStruct((HEADS * 8, DK), f32),
            jax.ShapeDtypeStruct((HEADS * DV, DK), f32),
            jax.ShapeDtypeStruct((HEADS * DV, DK), f32),
        ],
        cost_estimate=pl.CostEstimate(
            flops=4 * work, bytes_accessed=length * HEADS * 24 * DK, transcendentals=0
        ),
        name="states",
    )(*rows)
    chunks = HEADS * DV // ROWS
    vmem = pl.BlockSpec(memory_space=pltpu.VMEM)
    incoming, outgoing = pl.pallas_call(
        functools.partial(chain_kernel, count),
        in_specs=[vmem] * 3,
        out_specs=[vmem] * 2,
        out_shape=[jax.ShapeDtypeStruct((HEADS * DV, DK), f32)] * 2,
        scratch_shapes=[pltpu.VMEM((HEADS * DV, DK), f32)] * 2
        + [pltpu.SemaphoreType.DMA((chunks,))] * 4,
        compiler_params=pltpu.CompilerParams(collective_id=0, has_side_effects=True),
        name="chain",
    )(decay, forward, backward)
    grad_q, grad_k, grad_v, grad_gate = pl.pallas_call(
        grads_kernel,
        grid=(HEADS,),
        in_specs=[thin, thin, wide, wide, thin, carry, carry],
        out_specs=[thin, thin, wide, thin],
        out_shape=[
            jax.ShapeDtypeStruct((length, HEADS * DK), bf16),
            jax.ShapeDtypeStruct((length, HEADS * DK), bf16),
            jax.ShapeDtypeStruct((length, HEADS * DV), bf16),
            jax.ShapeDtypeStruct((length, HEADS * DK), f32),
        ],
        scratch_shapes=[pltpu.VMEM((length, DK), f32)],
        cost_estimate=pl.CostEstimate(
            flops=16 * work, bytes_accessed=length * HEADS * 40 * DK, transcendentals=0
        ),
        name="grads",
    )(*rows, incoming, outgoing)
    grad_key_weight = lax.psum_scatter(
        lax.dot_general(layer_input[0], grad_k, TN, preferred_element_type=f32),
        ("dp", "seq"),
        scatter_dimension=0,
        tiled=True,
    )
    return (grad_q[None], grad_k[None], grad_v[None], grad_gate[None], grad_key_weight)


def solution(mesh):
    rows = P("dp", "seq", None)
    return jax.shard_map(
        functools.partial(shards, mesh.shape["seq"]),
        mesh=mesh,
        in_specs=(rows,) * 6,
        out_specs=(rows, rows, rows, rows, P(("dp", "seq"), None)),
        check_vma=False,
    )
```

time: 684 us -> 393 us (0.57)
  matrix products: 179 us -> 6.83 us
  Pallas kernels: 0 us -> 153 us
  local copies, waits for them, and re-layouts: 102 us -> 9.25 us
  blocking collectives: 77.9 us -> 0 us
  other arithmetic: 49.4 us -> 0 us
  waiting for transfers between devices: 257 us -> 209 us
    all_gather x2 -> x0, waiting for transfers between devices: 235 us -> none  [carried_in(): gathered = jax.tree.map(lambda a: lax.all_gather(a, axis), part)]
    unnamed x4 -> x2, waiting for transfers between devices: 21.8 us -> 209 us
    dot_general x67 -> x1, matrix products: 179 us -> 6.83 us  [shards(): lax.dot_general(layer_input[0], grad_k, TN, preferred_element_type=f32)]
    pallas_call x0 -> x3, Pallas kernels: none -> 153 us  [the longest x1 130 us: shards(): pl.pallas_call(functools.partial(chain_kernel, count), in_specs=[vmem] *...]
    all_gather x2 -> x0, blocking collectives: 77.9 us -> none  [carried_in(): gathered = jax.tree.map(lambda a: lax.all_gather(a, axis), part)]
    add x17 -> x0, other arithmetic: 32.4 us -> none  [the longest x7 27.5 us: chained(): decay_late[..., None] * state_early + state_late]
    dynamic_slice x24 -> x0, local copies, waits for them, and re-layouts: 23.1 us -> none  [forward_blocks(): lax.scan(forward_advance, start_state, (key_rows, value_rows, cotan_rows,...]
    another operation x7 -> x0, local copies, waits for them, and re-layouts: 19.5 us -> none  [the longest x5 16.4 us: as_blocks(): return array[0].reshape(blocks, GROUP, HEADS, width)]
  transfers between devices with their start and end apart: 3 -> 1, of which waited for: 3 -> 1; matrix products, arithmetic and copies ran while one was open for 45% -> 0% of each run, Pallas kernels for 0% -> 0%
where the time goes in v1:
time: 393 us; the launch traced here: 392 us
  waiting for transfers between devices  209 us (53%)
  Pallas kernels  153 us (39%)
  between operations  14 us (4%)
  local copies, waits for them, and re-layouts  9.25 us (2%)
  matrix products  6.83 us (2%)
    unnamed x2, waiting for transfers between devices  209 us
    pallas_call x1, Pallas kernels, shards(): pl.pallas_call(functools.partial(chain_kernel, count), in_specs=[vmem] *...  130 us
    pallas_call x1, Pallas kernels, shards(): pl.pallas_call(grads_kernel, grid=(HEADS,), in_specs=[thin, thin, wide, w...  15.3 us
    unnamed x3, local copies, waits for them, and re-layouts  9.25 us
  transfers between devices with their start and end apart: 1, of which 1 were waited for; matrix products, arithmetic and copies ran while one was open for 0% of the time, Pallas kernels for 0%

profile of v1, /device:TPU:1, one launch (start us, length us, event | category | flops | bytes accessed | tf_op | source)
XLA Modules:
  0.0 392.3 jit_solution(17332399688224102922)
XLA Ops:
  7.2 0.0 copy-start
  7.2 0.0 reduce-scatter.4.cloned.1.call-start
  7.2 7.6 %states.1 = (f32[32,256]{1,0:T(8,128)}, f32[2048,256]{1,0:T(8,128)}, f32[2048,256]{1,0:T(8,128)}) custom-call(bf16[512,1024]{1,0:T(8,128)(2,1)} %bitcast.22, bf16[512,1024]{1,0:T(8,128)(2,1)} %bitcast.24, bf16[512,2048]{1,0:T(8,128)(2,1)} %bitcast.16, bf16[512,2048]{1,0:T(8,128)(2,1)} %bitcast.18, f32[512,1024]{1,0:T(8,128)} %bitcast.20), custom_call_target="tpu_custom_call" | custom-call | flops 1073741824 | bytes 12582912 | tf_op jit(solution)/shard_map/states/pallas_call | solution.py:200
  14.8 130.1 %chain.1 = (f32[2048,256]{1,0:T(8,128)}, f32[2048,256]{1,0:T(8,128)}) custom-call(f32[32,256]{1,0:T(8,128)} %get-tuple-element.14.decay_ref, f32[2048,256]{1,0:T(8,128)} %get-tuple-element.15.f_ref, f32[2048,256]{1,0:T(8,128)} %get-tuple-element.16.b_ref), custom_call_target="tpu_custom_call" | custom-call | tf_op jit(solution)/shard_map/chain/pallas_call | solution.py:217
  144.9 15.3 %grads.1 = (bf16[512,1024]{1,0:T(8,128)(2,1)}, bf16[512,1024]{1,0:T(8,128)(2,1)}, bf16[512,2048]{1,0:T(8,128)(2,1)}, f32[512,1024]{1,0:T(8,128)}) custom-call(bf16[512,1024]{1,0:T(8,128)(2,1)} %bitcast.23, bf16[512,1024]{1,0:T(8,128)(2,1)} %bitcast.25, bf16[512,2048]{1,0:T(8,128)(2,1)} %bitcast.17, bf16[512,2048]{1,0:T(8,128)(2,1)} %bitcast.19, ...), custom_call_target="tpu_custom_call" | custom-call | flops 4294967296 | bytes 20971520 | tf_op jit(solution)/shard_map/grads/pallas_call | solution.py:227
  160.2 0.0 copy-done
  160.2 6.8 %convolution_bitcast_fusion = f32[2048,1024]{0,1:T(8,128)} fusion(bf16[512,1024]{1,0:T(8,128)(2,1)} %get-tuple-element.20, bf16[1,512,2048]{2,1,0:T(8,128)(2,1)S(1)} %copy-done), kind=kOutput, calls=%fused_computation | convolution fusion | flops 2147483648 | bytes 11534336 | tf_op jit(solution)/shard_map/dot_general | solution.py:245
  167.0 9.2 %copy.13 = f32[2048,1024]{1,0:T(8,128)} copy(f32[2048,1024]{0,1:T(8,128)} %convolution_bitcast_fusion) | data formatting | bytes 16777216
  176.3 0.0 reduce-scatter.4.cloned.1.call-update
  176.3 209.2 %reduce-scatter.4.cloned.1.call-done = f32[64,1024]{1,0:T(8,128)} async-done(((f32[2048,1024]{1,0:T(8,128)}), f32[64,1024]{1,0:T(8,128)}) %reduce-scatter.4.cloned.1.call-update) | async-done | bytes 262160
Async XLA Ops:
  7.2 153.0 %copy-start = (bf16[1,512,2048]{2,1,0:T(8,128)(2,1)S(1)}, bf16[1,512,2048]{2,1,0:T(8,128)(2,1)}, u32[]{:S(2)}) copy-start(bf16[1,512,2048]{2,1,0:T(8,128)(2,1)} %param.11) | copy-start | bytes 6291460
  7.2 378.3 %reduce-scatter.4.cloned.1.call-start = ((), (), s32[]{:S(2)}) async-start(), calls=%async_computation.1 | async-start | bytes 8650752
Sparse Core Ops, SparseCore 0:
  176.4 208.9 reduce-scatter.3

commit v2 on v1

--- a/solution.py
+++ b/solution.py
@@ -11,6 +11,7 @@
 DK = 256
 DV = 512
 ROWS = 64
+LANES = 128
 NT = (((1,), (1,)), ((), ()))
 TN = (((0,), (0,)), ((), ()))
 NN = (((1,), (0,)), ((), ()))
@@ -189,8 +190,165 @@
         )
 
 
-def shards(count, queries, key_vectors, value_vectors, grad_output, log_gate, layer_input):
+def weight_kernel(x_ref, k_ref, out_ref):
+    total = mm(x_ref[...], k_ref[...], TN)
+    for c in range(out_ref.shape[0]):
+        out_ref[c] = total[:, c * LANES : (c + 1) * LANES]
+
+
+def scatter_kernel(sizes, part_ref, out_ref, *scratch):
+    wide, high, low = sizes
+    r0, s0, ry1, sy1, ry2, rb1, sb1, rb2, s2, r3, send, recv = scratch
+    chunks = part_ref.shape[0]
+    dp, seq = lax.axis_index("dp"), lax.axis_index("seq")
+    y, core = dp // 2, dp % 2
+    a, b = seq // low, seq % low
+    other = 1 - core
+
+    def peers(axis):
+        me, size = {"y": (y, wide), "b": (b, low), "a": (a, high)}[axis]
+        return [lax.rem(me + k, size) for k in range(1, size)]
+
+    def device(axis, value):
+        place = {"y": y, "core": core, "a": a, "b": b} | {axis: value}
+        return {"dp": place["y"] * 2 + place["core"], "seq": place["a"] * low + place["b"]}
+
+    barrier = pltpu.get_barrier_semaphore()
+    reached = [device("core", other)]
+    for axis in ("y", "b", "a"):
+        reached += [device(axis, p) for p in peers(axis)]
+    for target in reached:
+        pl.semaphore_signal(
+            barrier, inc=1, device_id=target, device_id_type=pl.DeviceIdType.MESH
+        )
+    pl.semaphore_wait(barrier, len(reached))
+
+    def copies(c, stage, axis, source, into):
+        made = []
+        for k, peer in enumerate([other] if axis == "core" else peers(axis)):
+            made.append(
+                pltpu.make_async_remote_copy(
+                    src_ref=source(peer),
+                    dst_ref=into(k),
+                    send_sem=send.at[stage, c, k],
+                    recv_sem=recv.at[stage, c, k],
+                    device_id=device(axis, peer),
+                    device_id_type=pl.DeviceIdType.MESH,
+                )
+            )
+        return made
+
+    def stage_of(c, stage):
+        half = c // 2
+        y_first = c % 2 == 0
+        if stage == 0:
+            return copies(c, 0, "core", lambda p: part_ref.at[c, :, p], lambda k: r0.at[c])
+        if stage == 1 and y_first:
+            return copies(c, 1, "y", lambda p: s0.at[c, p], lambda k: ry1.at[half, k])
+        if stage == 1:
+            return copies(c, 1, "b", lambda p: s0.at[c, :, :, p], lambda k: rb1.at[half, k])
+        if stage == 2 and y_first:
+            return copies(c, 2, "b", lambda p: sy1.at[half, :, p], lambda k: ry2.at[half, k])
+        if stage == 2:
+            return copies(c, 2, "y", lambda p: sb1.at[half, p], lambda k: rb2.at[half, k])
+        return copies(c, 3, "a", lambda p: s2.at[c, p], lambda k: r3.at[c, k])
+
+    def landed(c, stage):
+        half = c // 2
+        y_first = c % 2 == 0
+        for one in stage_of(c, stage):
+            one.wait_recv()
+        if stage == 0:
+            s0[c] = part_ref[c, :, core] + r0[c]
+        elif stage == 1 and y_first:
+            sy1[half] = sum((ry1[half, k] for k in range(wide - 1)), s0[c, y])
+        elif stage == 1:
+            sb1[half] = sum((rb1[half, k] for k in range(low - 1)), s0[c, :, :, b])
+        elif stage == 2 and y_first:
+            s2[c] = sum((ry2[half, k] for k in range(low - 1)), sy1[half, :, b])
+        elif stage == 2:
+            s2[c] = sum((rb2[half, k] for k in range(wide - 1)), sb1[half, y])
+        else:
+            out_ref[:, c * LANES : (c + 1) * LANES] = sum(
+                (r3[c, k] for k in range(high - 1)), s2[c, a]
+            )
+
+    def begin(c, stage):
+        for one in stage_of(c, stage):
+            one.start()
+
+    for c in range(chunks):
+        begin(c, 0)
+    for c in range(chunks):
+        landed(c, 0)
+        begin(c, 1)
+    for t in range(chunks + 2):
+        for stage in (1, 2, 3):
+            c = t - stage + 1
+            if 0 <= c < chunks:
+                landed(c, stage)
+                if stage < 3:
+                    begin(c, stage + 1)
+    for c in range(chunks):
+        for stage in range(4):
+            for one in stage_of(c, stage):
+                one.wait_send()
+
+
+def weight_sum(counts, layer_rows, grad_k):
+    length, model = layer_rows.shape
+    columns = grad_k.shape[1]
+    ranks, count = counts
+    chunks = columns // LANES
+    tall = min(256, model)
+    part = pl.pallas_call(
+        weight_kernel,
+        grid=(model // tall,),
+        in_specs=[
+            pl.BlockSpec((length, tall), lambda i: (0, i)),
+            pl.BlockSpec((length, columns), lambda i: (0, 0)),
+        ],
+        out_specs=pl.BlockSpec((chunks, tall, LANES), lambda i: (0, i, 0)),
+        out_shape=jax.ShapeDtypeStruct((chunks, model, LANES), jnp.float32),
+        name="weight",
+    )(layer_rows, grad_k)
+    low = max(d for d in range(1, count + 1) if count % d == 0 and d * d <= count)
+    high, wide = count // low, ranks // 2
+    rows = model // (ranks * count)
+    half = chunks // 2
+
+    def held(*lead):
+        return pltpu.VMEM(lead + (rows, LANES), jnp.float32)
+
+    most = max(wide, high, low)
+    vmem = pl.BlockSpec(memory_space=pltpu.VMEM)
+    return pl.pallas_call(
+        functools.partial(scatter_kernel, (wide, high, low)),
+        in_specs=[vmem],
+        out_specs=vmem,
+        out_shape=jax.ShapeDtypeStruct((rows, columns), jnp.float32),
+        scratch_shapes=[
+            held(chunks, wide, high, low),
+            held(chunks, wide, high, low),
+            held(half, wide - 1, high, low),
+            held(half, high, low),
+            held(half, low - 1, high),
+            held(half, low - 1, wide, high),
+            held(half, wide, high),
+            held(half, wide - 1, high),
+            held(chunks, high),
+            held(chunks, high - 1),
+            pltpu.SemaphoreType.DMA((4, chunks, most - 1)),
+            pltpu.SemaphoreType.DMA((4, chunks, most - 1)),
+        ],
+        compiler_params=pltpu.CompilerParams(collective_id=1, has_side_effects=True),
+        name="scatter",
+    )(part.reshape(chunks, wide, 2, high, low, rows, LANES))
+
+
+def shards(counts, queries, key_vectors, value_vectors, grad_output, log_gate, layer_input):
     length = queries.shape[1]
+    count = counts[1]
     f32, bf16 = jnp.float32, jnp.bfloat16
     thin = pl.BlockSpec((length, DK), lambda h: (0, h))
     wide = pl.BlockSpec((length, DV), lambda h: (0, h))
@@ -241,19 +399,14 @@
         ),
         name="grads",
     )(*rows, incoming, outgoing)
-    grad_key_weight = lax.psum_scatter(
-        lax.dot_general(layer_input[0], grad_k, TN, preferred_element_type=f32),
-        ("dp", "seq"),
-        scatter_dimension=0,
-        tiled=True,
-    )
+    grad_key_weight = weight_sum(counts, layer_input[0], grad_k)
     return (grad_q[None], grad_k[None], grad_v[None], grad_gate[None], grad_key_weight)
 
 
 def solution(mesh):
     rows = P("dp", "seq", None)
     return jax.shard_map(
-        functools.partial(shards, mesh.shape["seq"]),
+        functools.partial(shards, (mesh.shape["dp"], mesh.shape["seq"])),
         mesh=mesh,
         in_specs=(rows,) * 6,
         out_specs=(rows, rows, rows, rows, P(("dp", "seq"), None)),

time: 393 us -> 251 us (0.64)
  waiting for transfers between devices: 209 us -> 0 us
  Pallas kernels: 153 us -> 246 us
  between operations: 14 us -> 0.65 us
  local copies, waits for them, and re-layouts: 9.25 us -> 1.67 us
  matrix products: 6.83 us -> 0 us
    unnamed x2 -> x0, waiting for transfers between devices: 209 us -> none
    pallas_call x0 -> x2, Pallas kernels: none -> 93.2 us  [the longest x1 84.6 us: weight_sum(): pl.pallas_call(functools.partial(scatter_kernel, (wide, high, low)), in_s...]
    unnamed x3 -> x1, local copies, waits for them, and re-layouts: 9.25 us -> 1.67 us
    dot_general x1 -> x0, matrix products: 6.83 us -> none  [shards(): lax.dot_general(layer_input[0], grad_k, TN, preferred_element_type=f32)]
  transfers between devices with their start and end apart: 1 -> 0, of which waited for: 1 -> 0; matrix products, arithmetic and copies ran while one was open for 0% -> 0% of each run, Pallas kernels for 0% -> 0%
where the time goes in v2:
time: 251 us; the launch traced here: 248 us
  Pallas kernels  246 us (98%)
    pallas_call x1, Pallas kernels, shards(): pl.pallas_call(functools.partial(chain_kernel, count), in_specs=[vmem] *...  130 us
    pallas_call x1, Pallas kernels, weight_sum(): pl.pallas_call(functools.partial(scatter_kernel, (wide, high, low)), in_s...  84.6 us
    pallas_call x1, Pallas kernels, shards(): pl.pallas_call(grads_kernel, grid=(HEADS,), in_specs=[thin, thin, wide, w...  15.2 us
    pallas_call x1, Pallas kernels, weight_sum(): pl.pallas_call(weight_kernel, grid=(model // tall,), in_specs=[pl.BlockSp...  8.62 us
    pallas_call x1, Pallas kernels, shards(): pl.pallas_call(states_kernel, grid=(HEADS,), in_specs=[thin, thin, wide,...  7.43 us

profile of v2, /device:TPU:1, one launch (start us, length us, event | category | flops | bytes accessed | tf_op | source)
XLA Modules:
  0.0 248.3 jit_solution(1727972994268556419)
XLA Ops:
  0.6 7.4 %states.1 = (f32[32,256]{1,0:T(8,128)}, f32[2048,256]{1,0:T(8,128)}, f32[2048,256]{1,0:T(8,128)}) custom-call(bf16[512,1024]{1,0:T(8,128)(2,1)} %bitcast.19, bf16[512,1024]{1,0:T(8,128)(2,1)} %bitcast.21, bf16[512,2048]{1,0:T(8,128)(2,1)} %bitcast.12, bf16[512,2048]{1,0:T(8,128)(2,1)} %bitcast.14, f32[512,1024]{1,0:T(8,128)} %bitcast.16), custom_call_target="tpu_custom_call" | custom-call | flops 1073741824 | bytes 12582912 | tf_op jit(solution)/shard_map/states/pallas_call | solution.py:358
  8.1 130.1 %chain.1 = (f32[2048,256]{1,0:T(8,128)}, f32[2048,256]{1,0:T(8,128)}) custom-call(f32[32,256]{1,0:T(8,128)} %get-tuple-element.14.decay_ref, f32[2048,256]{1,0:T(8,128)} %get-tuple-element.15.f_ref, f32[2048,256]{1,0:T(8,128)} %get-tuple-element.16.b_ref), custom_call_target="tpu_custom_call" | custom-call | tf_op jit(solution)/shard_map/chain/pallas_call | solution.py:375
  138.1 15.2 %grads.1 = (bf16[512,1024]{1,0:T(8,128)(2,1)}, bf16[512,1024]{1,0:T(8,128)(2,1)}, bf16[512,2048]{1,0:T(8,128)(2,1)}, f32[512,1024]{1,0:T(8,128)}) custom-call(bf16[512,1024]{1,0:T(8,128)(2,1)} %bitcast.20, bf16[512,1024]{1,0:T(8,128)(2,1)} %bitcast.22, bf16[512,2048]{1,0:T(8,128)(2,1)} %bitcast.13, bf16[512,2048]{1,0:T(8,128)(2,1)} %bitcast.15, ...), custom_call_target="tpu_custom_call" | custom-call | flops 4294967296 | bytes 20971520 | tf_op jit(solution)/shard_map/grads/pallas_call | solution.py:385
  153.4 8.6 %weight.1 = f32[8,2048,128]{2,1,0:T(8,128)} custom-call(bf16[512,2048]{1,0:T(8,128)(2,1)} %bitcast.18, bf16[512,1024]{1,0:T(8,128)(2,1)} %get-tuple-element.20.k_ref), custom_call_target="tpu_custom_call" | custom-call | tf_op jit(solution)/shard_map/weight/pallas_call | solution.py:304
  162.0 84.6 %scatter.1 = f32[64,1024]{1,0:T(8,128)} custom-call(f32[8,2,2,4,2,64,128]{6,5,4,3,2,1,0:T(8,128)} %bitcast.11), custom_call_target="tpu_custom_call" | custom-call | tf_op jit(solution)/shard_map/scatter/pallas_call | solution.py:325
  246.6 1.7 copy.12

commit v3 on v2

--- a/solution.py
+++ b/solution.py
@@ -11,6 +11,7 @@
 DK = 256
 DV = 512
 ROWS = 64
+SLACK = 3
 LANES = 128
 NT = (((1,), (1,)), ((), ()))
 TN = (((0,), (0,)), ((), ()))
@@ -108,8 +109,8 @@
     at_low, at_high = place == 0, place == count - 1
 
     def step(t, _):
-        ahead = t - place
-        back = t - (count - 1 - place)
+        ahead = t - SLACK * place
+        back = t - SLACK * (count - 1 - place)
 
         @pl.when((ahead >= 0) & (ahead < chunks))
         def _():
@@ -121,7 +122,7 @@
 
         return 0
 
-    lax.fori_loop(0, chunks + count - 1, step, 0)
+    lax.fori_loop(0, chunks + SLACK * (count - 1), step, 0)
 
     def drain(c, _):
         @pl.when(jnp.logical_not(at_high))

time: 251 us -> 218 us (0.87)
  Pallas kernels: 246 us -> 212 us
    pallas_call x1, Pallas kernels: 84.6 us -> 62.2 us  [weight_sum(): pl.pallas_call(functools.partial(scatter_kernel, (wide, high, low)), in_s...]
    pallas_call x1, Pallas kernels: 130 us -> 119 us  [shards(): pl.pallas_call(functools.partial(chain_kernel, count), in_specs=[vmem] *...]
where the time goes in v3:
time: 218 us; the launch traced here: 215 us
  Pallas kernels  212 us (97%)
    pallas_call x1, Pallas kernels, shards(): pl.pallas_call(functools.partial(chain_kernel, count), in_specs=[vmem] *...  119 us
    pallas_call x1, Pallas kernels, weight_sum(): pl.pallas_call(functools.partial(scatter_kernel, (wide, high, low)), in_s...  62.2 us
    pallas_call x1, Pallas kernels, shards(): pl.pallas_call(grads_kernel, grid=(HEADS,), in_specs=[thin, thin, wide, w...  15.2 us
    pallas_call x1, Pallas kernels, weight_sum(): pl.pallas_call(weight_kernel, grid=(model // tall,), in_specs=[pl.BlockSp...  8.62 us
    pallas_call x1, Pallas kernels, shards(): pl.pallas_call(states_kernel, grid=(HEADS,), in_specs=[thin, thin, wide,...  7.43 us

profile of v3, /device:TPU:1, one launch (start us, length us, event | category | flops | bytes accessed | tf_op | source)
XLA Modules:
  0.0 214.5 jit_solution(9982973703948708160)
XLA Ops:
  0.6 7.4 %states.1 = (f32[32,256]{1,0:T(8,128)}, f32[2048,256]{1,0:T(8,128)}, f32[2048,256]{1,0:T(8,128)}) custom-call(bf16[512,1024]{1,0:T(8,128)(2,1)} %bitcast.19, bf16[512,1024]{1,0:T(8,128)(2,1)} %bitcast.21, bf16[512,2048]{1,0:T(8,128)(2,1)} %bitcast.12, bf16[512,2048]{1,0:T(8,128)(2,1)} %bitcast.14, f32[512,1024]{1,0:T(8,128)} %bitcast.16), custom_call_target="tpu_custom_call" | custom-call | flops 1073741824 | bytes 12582912 | tf_op jit(solution)/shard_map/states/pallas_call | solution.py:359
  8.1 118.7 %chain.1 = (f32[2048,256]{1,0:T(8,128)}, f32[2048,256]{1,0:T(8,128)}) custom-call(f32[32,256]{1,0:T(8,128)} %get-tuple-element.14.decay_ref, f32[2048,256]{1,0:T(8,128)} %get-tuple-element.15.f_ref, f32[2048,256]{1,0:T(8,128)} %get-tuple-element.16.b_ref), custom_call_target="tpu_custom_call" | custom-call | tf_op jit(solution)/shard_map/chain/pallas_call | solution.py:376
  126.8 15.2 %grads.1 = (bf16[512,1024]{1,0:T(8,128)(2,1)}, bf16[512,1024]{1,0:T(8,128)(2,1)}, bf16[512,2048]{1,0:T(8,128)(2,1)}, f32[512,1024]{1,0:T(8,128)}) custom-call(bf16[512,1024]{1,0:T(8,128)(2,1)} %bitcast.20, bf16[512,1024]{1,0:T(8,128)(2,1)} %bitcast.22, bf16[512,2048]{1,0:T(8,128)(2,1)} %bitcast.13, bf16[512,2048]{1,0:T(8,128)(2,1)} %bitcast.15, ...), custom_call_target="tpu_custom_call" | custom-call | flops 4294967296 | bytes 20971520 | tf_op jit(solution)/shard_map/grads/pallas_call | solution.py:386
  142.0 8.6 %weight.1 = f32[8,2048,128]{2,1,0:T(8,128)} custom-call(bf16[512,2048]{1,0:T(8,128)(2,1)} %bitcast.18, bf16[512,1024]{1,0:T(8,128)(2,1)} %get-tuple-element.20.k_ref), custom_call_target="tpu_custom_call" | custom-call | tf_op jit(solution)/shard_map/weight/pallas_call | solution.py:305
  150.6 62.2 %scatter.1 = f32[64,1024]{1,0:T(8,128)} custom-call(f32[8,2,2,4,2,64,128]{6,5,4,3,2,1,0:T(8,128)} %bitcast.11), custom_call_target="tpu_custom_call" | custom-call | tf_op jit(solution)/shard_map/scatter/pallas_call | solution.py:326
  212.9 1.7 copy.12
